TPU v7x, 32 devices: a whole 2x2x4 slice. The times are simulated.
32 devices in a mesh: blk: 16 (over z, y, core), along: 2 (over x).
Axes of the slice: x: 2, y: 2, z: 4, core: 2. Of those that a mesh axis runs over, the one named last changes fastest.
Arguments:
- values: float32 [3, 16, 48, 256], P(None, 'blk', 'along'), may hold values from -6 to 6
- offsets: float32 [3, 16, 48, 256], P(None, 'blk', 'along'), may hold values from 0 to 1
- stiffness: float32 [16, 48, 256], P('blk', 'along'), may hold values from 0.5 to 2
- leaf_basis: float32 [16, 48, 64, 256], P('blk', 'along'), may hold values from -0.375 to 0.375
- transfer: float32 [16, 48, 64, 64], P('blk', 'along'), may hold values from -0.15625 to 0.15625
- slab_transfer_matrices: float32 [16, 2, 64, 64], P('blk', 'along'), may hold values from -0.5 to 0.5
- leaf_coupling_matrices: float32 [16, 30, 64, 64], P('blk'), may hold values from -0.375 to 0.375
- leaf_admissible_mask: int32 [16, 30], P('blk'), may hold values 0 or 1
- top_coupling: float32 [16, 16, 64, 64], P('blk'), may hold values from -0.75 to 0.75
- top_admissible: int32 [16, 16], P('blk'), may hold values 0 or 1
Outputs:
- product: float32 [3, 16, 48, 256], P(None, 'blk', 'along')
All inputs are finite; a program needn't handle non-finite values. No bound on the sum of `leaf_admissible_mask` or of `top_admissible` on one device may be relied on, other than what follows from the above.
Results may differ from a plain program's by a relative error of at most 0.0001.
Values sent between devices are 32-bit elements; how exact they have to be, the bound alone decides.
A program may use at most 64 MiB of HBM per device.

v0:
```python
import jax
import jax.numpy as jnp
from jax import lax
from jax.sharding import PartitionSpec as P

REACH = 6
SHARPNESS = 2.0
KERNEL_SCALE = 0.125
HIGHEST_ACCURACY = lax.Precision.HIGHEST


def with_halo(cells, sides, width, closed):
    for axis, dim in sides:
        count = lax.axis_size(axis)
        ends = count if closed else count - 1
        head = lax.slice_in_dim(cells, 0, width, axis=dim)
        tail = lax.slice_in_dim(cells, cells.shape[dim] - width, cells.shape[dim], axis=dim)
        cells = jnp.concatenate(
            [
                lax.ppermute(tail, axis, [(i, (i + 1) % count) for i in range(ends)]),
                cells,
                lax.ppermute(head, axis, [((i + 1) % count, i) for i in range(ends)]),
            ],
            axis=dim,
        )
    return cells


def passed_along(x, axis, by):
    count = lax.axis_size(axis)
    return lax.ppermute(x, axis, [(i, (i + by) % count) for i in range(count)])


def near_field(padded):
    leaves = padded.shape[2] - 2
    center = padded[:, 1:2, 1 : 1 + leaves]
    result = jnp.zeros((3, 1, leaves, padded.shape[3]), jnp.float32)
    for around in (-1, 0, 1):
        for along_step in (-1, 0, 1):
            source = padded[:, 1 + around : 2 + around, 1 + along_step : 1 + along_step + leaves]
            gap_around = around + source[0][..., None, :] - center[0][..., :, None]
            gap_along = along_step + source[1][..., None, :] - center[1][..., :, None]
            gap_radial = source[2][..., None, :] - center[2][..., :, None]
            squared = gap_around * gap_around + gap_along * gap_along + gap_radial * gap_radial
            kernel = (
                KERNEL_SCALE
                * center[3][..., :, None]
                * source[3][..., None, :]
                * jnp.exp(-SHARPNESS * squared)
            )
            result = result + jnp.einsum(
                "alij,ralj->rali", kernel, source[4:], precision=HIGHEST_ACCURACY
            )
    return result


def slot_number(around, along_step, reach):
    block = around - 2 if around > 0 else reach - 1 + (-around - 2)
    return 3 * block + along_step + 1


def add_sector(total, held, around, leaf_coupling_matrices, leaf_admissible_mask):
    leaves = total.shape[2]
    for along_step in (-1, 0, 1):
        slot = slot_number(around, along_step, REACH)
        partner = held[:, :, 1 + along_step : 1 + along_step + leaves]
        coupling = (
            leaf_coupling_matrices[:, slot]
            * leaf_admissible_mask[:, slot].astype(jnp.float32)[:, None, None]
        )
        total = total + jnp.einsum("skq,rslq->rslk", coupling, partner, precision=HIGHEST_ACCURACY)
    return total


def body(
    values,
    offsets,
    stiffness,
    leaf_basis,
    transfer,
    slab_transfer_matrices,
    leaf_coupling_matrices,
    leaf_admissible_mask,
    top_coupling,
    top_admissible,
):
    stacked = jnp.concatenate([offsets, stiffness[None], values], 0)
    padded = with_halo(stacked, (("blk", 1), ("along", 2)), 1, True)
    at_start = lax.axis_index("along") == 0
    at_finish = lax.axis_index("along") == lax.axis_size("along") - 1
    lower_rim = jnp.where(at_start, 0.0, padded[:, :, :1])
    upper_rim = jnp.where(at_finish, 0.0, padded[:, :, -1:])
    padded = jnp.concatenate([lower_rim, padded[:, :, 1:-1], upper_rim], 2)
    near = near_field(padded)
    coefs = jnp.einsum("slki,rsli->rslk", leaf_basis, values, precision=HIGHEST_ACCURACY)
    rimmed = with_halo(coefs, (("along", 2),), 1, False)
    far_leaf = jnp.zeros(coefs.shape, jnp.float32)
    sectors = lax.axis_size("blk")
    lower_window = rimmed
    upper_window = rimmed
    breadth = 1
    while breadth <= REACH:
        lower_came = passed_along(lower_window, "blk", breadth)
        upper_came = passed_along(upper_window, "blk", -breadth)
        lower_window = jnp.concatenate([lower_window, lower_came], 1)
        upper_window = jnp.concatenate([upper_window, upper_came], 1)
        breadth = 2 * breadth
    for distance in range(2, REACH + 1):
        far_leaf = add_sector(
            far_leaf,
            lower_window[:, distance : distance + 1],
            -distance,
            leaf_coupling_matrices,
            leaf_admissible_mask,
        )
        far_leaf = add_sector(
            far_leaf,
            upper_window[:, distance : distance + 1],
            distance,
            leaf_coupling_matrices,
            leaf_admissible_mask,
        )
    slab_coefficient_rows = jnp.einsum(
        "slqk,rslq->rsk", transfer, coefs, precision=HIGHEST_ACCURACY
    )
    shared_portion = jnp.einsum(
        "oxz,eox->eoz",
        slab_transfer_matrices[:, 0],
        slab_coefficient_rows,
        precision=HIGHEST_ACCURACY,
    )
    sector_coefs = lax.psum(shared_portion, "along")
    every_sector = lax.all_gather(sector_coefs, "blk", axis=1, tiled=True)
    sector = lax.axis_index("blk")
    others = jnp.arange(sectors, dtype=jnp.int32)
    apart = (others - sector) % sectors
    distant = jnp.logical_and(apart > REACH, apart < sectors - REACH).astype(jnp.float32)
    allowed = top_admissible[0].astype(jnp.float32) * distant
    sector_local_coefs = jnp.einsum(
        "stkq,rtq->rsk",
        top_coupling * allowed[None, :, None, None],
        every_sector,
        precision=HIGHEST_ACCURACY,
    )
    slab_local_coefs = jnp.einsum(
        "baz,lbz->lba", slab_transfer_matrices[:, 0], sector_local_coefs, precision=HIGHEST_ACCURACY
    )
    leaf_down = jnp.einsum("slqk,rsk->rslq", transfer, slab_local_coefs, precision=HIGHEST_ACCURACY)
    leaf_local = far_leaf + leaf_down
    return near + jnp.einsum("slki,rslk->rsli", leaf_basis, leaf_local, precision=HIGHEST_ACCURACY)


def solution(mesh):
    return jax.shard_map(
        body,
        mesh=mesh,
        in_specs=(
            P(None, "blk", "along", None),
            P(None, "blk", "along", None),
            P("blk", "along", None),
            P("blk", "along", None, None),
            P("blk", "along", None, None),
            P("blk", "along", None, None),
            P("blk", None, None, None),
            P("blk", None),
            P("blk", None, None, None),
            P("blk", None),
        ),
        out_specs=P(None, "blk", "along", None),
        check_vma=False,
    )
```

profile of v0, /device:TPU:0, one launch (start us, length us, event | category | flops | bytes accessed | tf_op | source)
XLA Modules:
  0.0 189.9 jit_solution(18029766824902312547)
XLA Ops:
  0.0 1.1 copy.17
  1.1 0.8 broadcast_in_dim.8
  1.9 0.9 copy.16
  2.8 0.7 pad_maximum_fusion.4
  3.5 5.5 %collective-permute-start.1 = (f32[7,1,24,256]{3,0,2,1:T(8,128)}, f32[7,1,24,256]{3,0,2,1:T(8,128)S(1)}, u32[]{:S(2)}, u32[]{:S(2)}) collective-permute-start(f32[7,1,24,256]{3,0,2,1:T(8,128)} %pad_maximum_fusion.4), channel_id=1, source_target_pairs={{2,0},{4,2},{6,4},{8,6},{10,8},{12,10},{14,12},{16,14},{18,16},{20... | collective-permute-start | bytes 516104 | tf_op jit(solution)/shard_map/ppermute | solution.py:22
  9.0 2.3 %fusion.200 = f32[24,3,64]{2,1,0:T(4,128)S(1)} fusion(f32[1,24,64,256]{3,2,1,0:T(8,128)S(1)} %copy-done, f32[3,24,256]{2,1,0:T(8,128)} %bitcast.397), kind=kOutput, calls=%fused_computation.200 | convolution fusion | flops 14155776 | bytes 1665024 | tf_op jit(solution)/shard_map/slki,rsli->rslk/dot_general | solution.py:95
  11.3 0.6 fusion.435
  11.9 1.3 collective-permute-start.5
  13.2 5.1 %collective-permute-start.4 = (f32[3,1,1,64]{3,0,2,1:T(4,128)}, f32[3,1,1,64]{3,0,2,1:T(4,128)}, u32[]{:S(2)}, u32[]{:S(2)}) collective-permute-start(f32[3,1,1,64]{3,0,2,1:T(4,128)} %get-tuple-element.78), channel_id=1, source_target_pairs={{0,1},{2,3},{4,5},{6,7},{8,9},{10,11},{12,13},{14,15},{16,17},{18,... | collective-permute-start | bytes 2312 | tf_op jit(solution)/shard_map/ppermute | solution.py:20
  18.3 0.6 slice_bitcast_fusion.48
  19.0 0.6 broadcast_multiply_fusion
  19.6 0.5 convolution_bitcast_fusion.3
  20.1 0.7 convolution_bitcast_fusion.2
  20.8 5.6 %psum.7 = f32[3,1,64]{2,0,1:T(4,128)} all-reduce(f32[3,1,64]{2,0,1:T(4,128)} %convolution_bitcast_fusion.2), channel_id=1, replica_groups=mesh['blk'=16,'along'=2] {'along'}, use_global_device_ids=true, to_apply=%region_0.1 | all-reduce | flops 192 | bytes 1536 | tf_op jit(solution)/shard_map/psum | solution.py:132
  26.5 19.9 %all_gather.3 = f32[3,16,64]{2,0,1:T(4,128)} all-gather(f32[3,1,64]{2,0,1:T(4,128)} %psum.7), channel_id=1, replica_groups=mesh['blk'=16,'along'=2] {'blk'}, dimensions={1}, use_global_device_ids=true | all-gather | bytes 13056 | tf_op jit(solution)/shard_map/all_gather | solution.py:133
  46.3 0.7 and_select_fusion
  47.0 1.3 convolution_bitcast_fusion
  48.3 0.9 convolution_bitcast_fusion.1
  49.3 0.7 pad_maximum_fusion.8
  50.0 0.4 collective-permute-start.6
  50.4 4.1 %collective-permute-start.8 = (f32[3,1,26,64]{3,0,2,1:T(4,128)S(1)}, f32[3,1,26,64]{3,0,2,1:T(4,128)S(1)}, u32[]{:S(2)}, u32[]{:S(2)}) collective-permute-start(f32[3,1,26,64]{3,0,2,1:T(4,128)S(1)} %pad_maximum_fusion.8), channel_id=1, source_target_pairs={{0,30},{2,0},{4,2},{6,4},{8,6},{10,8},{12,10},{14,12},{16,14},{18,... | collective-permute-start | bytes 59912 | tf_op jit(solution)/shard_map/ppermute | solution.py:31
  54.5 0.7 fusion.436
  55.2 1.1 collective-permute-done.6
  56.3 1.4 pad_maximum_fusion.5
  57.7 4.7 %collective-permute-start.9 = (f32[3,2,26,64]{3,0,2,1:T(4,128)S(1)}, f32[3,2,26,64]{3,0,2,1:T(4,128)S(1)}, u32[]{:S(2)}, u32[]{:S(2)}) collective-permute-start(f32[3,2,26,64]{3,0,2,1:T(4,128)S(1)} %get-tuple-element.77), channel_id=1, source_target_pairs={{0,28},{2,30},{4,0},{6,2},{8,4},{10,6},{12,8},{14,10},{16,12},{18,... | collective-permute-start | bytes 119816 | tf_op jit(solution)/shard_map/ppermute | solution.py:31
  62.4 0.7 fusion.437
  82.0 0.8 pad_maximum_fusion.1
  82.9 2.0 %collective-permute-start.10 = (f32[3,4,26,64]{3,0,2,1:T(4,128)S(1)}, f32[3,4,26,64]{3,0,2,1:T(4,128)S(1)}, u32[]{:S(2)}, u32[]{:S(2)}) collective-permute-start(f32[3,4,26,64]{3,0,2,1:T(4,128)S(1)} %get-tuple-element.74), channel_id=1, source_target_pairs={{0,8},{2,10},{4,12},{6,14},{8,16},{10,18},{12,20},{14,22},{16,24},... | collective-permute-start | bytes 239624 | tf_op jit(solution)/shard_map/ppermute | solution.py:31
  84.9 1.0 fusion.279
  85.9 0.2 fusion.281
  86.1 0.2 fusion.283
  86.4 0.2 fusion.285
  86.6 0.2 fusion.287
  86.8 0.2 fusion.289
  87.0 0.2 fusion.291
  87.3 0.2 fusion.293
  87.5 0.2 fusion.295
  87.7 0.2 fusion.297
  87.9 0.2 fusion.299
  88.1 0.2 fusion.301
  88.4 6.1 %collective-permute-done.11 = f32[3,4,26,64]{3,0,2,1:T(4,128)S(1)} collective-permute-done((f32[3,4,26,64]{3,0,2,1:T(4,128)S(1)}, f32[3,4,26,64]{3,0,2,1:T(4,128)S(1)}, u32[]{:S(2)}, u32[]{:S(2)}) %collective-permute-start.11) | collective-permute-done | bytes 79904 | tf_op jit(solution)/shard_map/ppermute | solution.py:31
  94.5 0.2 fusion.243
  94.7 0.2 fusion.245
  95.3 0.2 fusion.249
  95.5 0.2 fusion.251
  96.4 0.2 fusion.259
  96.6 0.2 fusion.261
  97.7 0.2 fusion.271
  97.9 0.2 fusion.273
  98.7 2.0 %convolution_add_fusion = f32[3,24,64]{2,0,1:T(4,128)S(1)} fusion(f32[3,64,1]{1,0,2:T(4,128)S(1)} %convolution_bitcast_fusion.1, f32[1,24,64,64]{3,2,1,0:T(8,128)S(1)} %copy-done.1, f32[3,24,64]{2,1,0:T(8,128)S(1)} %fusion.243, f32[3,24,64]{2,1,0:T(8,128)S(1)} %fusion.245, f32[3,24,64]{2,1,0:T(8,128)S(1)} %fusion.247, f32[3,24,64]{2,1,0:T(8,128)S(1)} %fusion.249, ...), kind=kOutput, calls=%fused_computation.213 | convolution fusion | flops 3677184 | bytes 965376 | tf_op jit(solution)/shard_map/slqk,rsk->rslq/dot_general | solution.py:148
  100.6 2.0 %collective-permute-start.2 = (f32[7,3,1,256]{3,0,2,1:T(8,128)S(1)}, f32[7,3,1,256]{3,0,2,1:T(8,128)S(1)}, u32[]{:S(2)}, u32[]{:S(2)}) collective-permute-start(f32[7,3,1,256]{3,0,2,1:T(8,128)S(1)} %get-tuple-element.31), channel_id=1, source_target_pairs={{0,1},{1,0},{2,3},{3,2},{4,5},{5,4},{6,7},{7,6},{8,9},{9,8},{10,11... | collective-permute-start | bytes 64520 | tf_op jit(solution)/shard_map/ppermute | solution.py:20
  102.9 1.6 collective-permute-done.2
  105.8 0.4 copy-done.10
  106.3 9.2 %fusion = f32[24,3,256]{2,1,0:T(4,128)S(1)} fusion(f32[24,256]{1,0:T(8,128)S(1)} %get-tuple-element.110, f32[24,256]{1,0:T(8,128)S(1)} %get-tuple-element.111, f32[24,256]{1,0:T(8,128)S(1)} %get-tuple-element.112, f32[24,256]{1,0:T(8,128)S(1)} %get-tuple-element.113, f32[24,256]{1,0:T(8,128)S(1)} %copy-done.11, f32[24,256]{1,0:T(8,128)S(1)} %copy-done.12, ...), kind=kOutput, calls=%fused_computation | convolution fusion | flops 73924608 | bytes 368640 | tf_op jit(solution)/shard_map/alij,ralj->rali/dot_general | solution.py:51
  115.5 9.1 %fusion.39 = f32[24,3,256]{2,1,0:T(4,128)S(1)} fusion(f32[24,256]{1,0:T(8,128)S(1)} %get-tuple-element.122, f32[24,256]{1,0:T(8,128)S(1)} %get-tuple-element.123, f32[24,256]{1,0:T(8,128)S(1)} %get-tuple-element.124, f32[24,256]{1,0:T(8,128)S(1)} %get-tuple-element.125, f32[24,256]{1,0:T(8,128)S(1)} %copy-done.11, f32[24,256]{1,0:T(8,128)S(1)} %copy-done.12, ...), kind=kOutput, calls=%fused_computation.39 | convolution fusion | flops 73924608 | bytes 368640 | tf_op jit(solution)/shard_map/alij,ralj->rali/dot_general | solution.py:51
  124.5 9.1 %fusion.26 = f32[24,3,256]{2,1,0:T(4,128)S(1)} fusion(f32[24,256]{1,0:T(8,128)S(1)} %get-tuple-element.114, f32[24,256]{1,0:T(8,128)S(1)} %get-tuple-element.115, f32[24,256]{1,0:T(8,128)S(1)} %get-tuple-element.118, f32[24,256]{1,0:T(8,128)S(1)} %get-tuple-element.119, f32[24,256]{1,0:T(8,128)S(1)} %copy-done.11, f32[24,256]{1,0:T(8,128)S(1)} %copy-done.12, ...), kind=kOutput, calls=%fused_computation.26 | convolution fusion | flops 73924608 | bytes 368640 | tf_op jit(solution)/shard_map/alij,ralj->rali/dot_general | solution.py:51
  133.6 9.1 %fusion.65 = f32[24,3,256]{2,1,0:T(4,128)S(1)} fusion(f32[24,256]{1,0:T(8,128)S(1)} %get-tuple-element.126, f32[24,256]{1,0:T(8,128)S(1)} %get-tuple-element.127, f32[24,256]{1,0:T(8,128)S(1)} %get-tuple-element.130, f32[24,256]{1,0:T(8,128)S(1)} %get-tuple-element.131, f32[24,256]{1,0:T(8,128)S(1)} %copy-done.11, f32[24,256]{1,0:T(8,128)S(1)} %copy-done.12, ...), kind=kOutput, calls=%fused_computation.65 | convolution fusion | flops 73924608 | bytes 368640 | tf_op jit(solution)/shard_map/alij,ralj->rali/dot_general | solution.py:51
  142.6 9.1 %fusion.78 = f32[24,3,256]{2,1,0:T(4,128)S(1)} fusion(f32[24,256]{1,0:T(8,128)S(1)} %get-tuple-element.134, f32[24,256]{1,0:T(8,128)S(1)} %get-tuple-element.135, f32[24,256]{1,0:T(8,128)S(1)} %get-tuple-element.136, f32[24,256]{1,0:T(8,128)S(1)} %get-tuple-element.137, f32[24,256]{1,0:T(8,128)S(1)} %copy-done.11, f32[24,256]{1,0:T(8,128)S(1)} %copy-done.12, ...), kind=kOutput, calls=%fused_computation.78 | convolution fusion | flops 73924608 | bytes 368640 | tf_op jit(solution)/shard_map/alij,ralj->rali/dot_general | solution.py:51
  151.7 9.1 %fusion.104 = f32[24,3,256]{2,1,0:T(4,128)S(1)} fusion(f32[24,256]{1,0:T(8,128)S(1)} %copy-done.11, f32[24,256]{1,0:T(8,128)S(1)} %get-tuple-element.133, f32[24,256]{1,0:T(8,128)S(1)} %copy-done.12, f32[24,256]{1,0:T(8,128)S(1)} %get-tuple-element.129, f32[24,256]{1,0:T(8,128)S(1)} %copy-done.10, f32[24,256]{1,0:T(8,128)S(1)} %get-tuple-element.121, ...), kind=kOutput, calls=%fused_computation.104 | convolution fusion | flops 73924608 | bytes 368640 | tf_op jit(solution)/shard_map/alij,ralj->rali/dot_general | solution.py:51
  160.8 9.1 %fusion.226 = f32[24,3,256]{2,1,0:T(4,128)S(1)} fusion(f32[24,3,256]{2,1,0:T(4,128)S(1)} %fusion.65, f32[24,3,256]{2,1,0:T(4,128)S(1)} %fusion.78, f32[24,3,256]{2,1,0:T(4,128)S(1)} %fusion.104, f32[24,256]{1,0:T(8,128)S(1)} %get-tuple-element.116, f32[24,256]{1,0:T(8,128)S(1)} %get-tuple-element.120, f32[24,256]{1,0:T(8,128)S(1)} %get-tuple-element.128, ...), kind=kOutput, calls=%fused_computation.210 | convolution fusion | flops 73979904 | bytes 663552 | tf_op jit(solution)/shard_map/alij,ralj->rali/dot_general | solution.py:51
  169.9 9.5 %fusion.217 = f32[24,3,256]{2,1,0:T(4,128)S(1)} fusion(f32[24,3,256]{2,1,0:T(4,128)S(1)} %fusion.26, f32[24,3,256]{2,1,0:T(4,128)S(1)} %fusion.39, f32[24,3,256]{2,1,0:T(4,128)S(1)} %fusion.226, f32[24,256]{1,0:T(8,128)S(1)} %copy-done.11, f32[24,256]{1,0:T(8,128)S(1)} %copy-done.12, f32[24,256]{1,0:T(8,128)S(1)} %copy-done.10, ...), kind=kOutput, calls=%fused_computation.207 | convolution fusion | flops 73979904 | bytes 491520 | tf_op jit(solution)/shard_map/alij,ralj->rali/dot_general | solution.py:51
  179.3 9.1 %fusion.232 = f32[24,3,256]{2,1,0:T(4,128)S(1)} fusion(f32[24,3,256]{2,1,0:T(4,128)S(1)} %fusion, f32[24,3,256]{2,1,0:T(4,128)S(1)} %fusion.217, f32[24,256]{1,0:T(8,128)S(1)} %get-tuple-element.138, f32[24,256]{1,0:T(8,128)S(1)} %get-tuple-element.139, f32[24,256]{1,0:T(8,128)S(1)} %get-tuple-element.140, f32[24,256]{1,0:T(8,128)S(1)} %get-tuple-element.141, ...), kind=kOutput, calls=%fused_computation.212 | convolution fusion | flops 73961472 | bytes 565248 | tf_op jit(solution)/shard_map/alij,ralj->rali/dot_general | solution.py:51
  188.4 0.9 fusion.205
  189.3 0.7 copy.20
  (82 shorter events, 3.9 us)
Async XLA Ops:
  0.0 9.0 %copy-start = (f32[1,24,64,256]{3,2,1,0:T(8,128)S(1)}, f32[1,24,64,256]{3,2,1,0:T(8,128)}, u32[]{:S(2)}) copy-start(f32[1,24,64,256]{3,2,1,0:T(8,128)} %param.13) | copy-start | bytes 4718596
  0.0 19.0 %copy-start.8 = (f32[1,24,256]{2,1,0:T(8,128)S(1)}, f32[1,24,256]{2,1,0:T(8,128)}, u32[]{:S(2)}) copy-start(f32[1,24,256]{2,1,0:T(8,128)} %param.12) | copy-start | bytes 73732
  0.0 18.3 %copy-start.6 = (f32[3,1,24,256]{3,2,1,0:T(8,128)S(1)}, f32[3,1,24,256]{3,2,1,0:T(8,128)}, u32[]{:S(2)}) copy-start(f32[3,1,24,256]{3,2,1,0:T(8,128)} %param.11) | copy-start | bytes 221188
  0.0 19.6 %copy-start.1 = (f32[1,24,64,64]{3,2,1,0:T(8,128)S(1)}, f32[1,24,64,64]{3,2,1,0:T(8,128)}, u32[]{:S(2)}) copy-start(f32[1,24,64,64]{3,2,1,0:T(8,128)} %param.14) | copy-start | bytes 1179652
  2.8 17.3 %copy-start.7 = (f32[1,1,64,64]{3,2,1,0:T(8,128)S(1)}, f32[1,1,64,64]{3,2,1,0:T(8,128)}, u32[]{:S(2)}) copy-start(f32[1,1,64,64]{3,2,1,0:T(8,128)} %param.15) | copy-start | bytes 49156
  2.8 44.2 %copy-start.3 = (f32[1,16,64,64]{3,2,1,0:T(8,128)S(1)}, f32[1,16,64,64]{3,2,1,0:T(8,128)}, u32[]{:S(2)}) copy-start(f32[1,16,64,64]{3,2,1,0:T(8,128)} %param.18) | copy-start | bytes 786436
  3.5 95.0 %collective-permute-start.1 = (f32[7,1,24,256]{3,0,2,1:T(8,128)}, f32[7,1,24,256]{3,0,2,1:T(8,128)S(1)}, u32[]{:S(2)}, u32[]{:S(2)}) collective-permute-start(f32[7,1,24,256]{3,0,2,1:T(8,128)} %pad_maximum_fusion.4), channel_id=1, source_target_pairs={{2,0},{4,2},{6,4},{8,6},{10,8},{12,10},{14,12},{16,14},{18,16},{20... | collective-permute-start | bytes 516104 | tf_op jit(solution)/shard_map/ppermute | solution.py:22
  9.0 89.5 %collective-permute-start = (f32[7,1,24,256]{3,0,2,1:T(8,128)}, f32[7,1,24,256]{3,0,2,1:T(8,128)S(1)}, u32[]{:S(2)}, u32[]{:S(2)}) collective-permute-start(f32[7,1,24,256]{3,0,2,1:T(8,128)} %pad_maximum_fusion.4), channel_id=1, source_target_pairs={{0,2},{2,4},{4,6},{6,8},{8,10},{10,12},{12,14},{14,16},{16,18},{18... | collective-permute-start | bytes 516104 | tf_op jit(solution)/shard_map/ppermute | solution.py:20
  9.0 45.4 %copy-start.4 = (s32[1,30]{1,0:T(1,128)S(1)}, s32[1,30]{1,0:T(1,128)}, u32[]{:S(2)}) copy-start(s32[1,30]{1,0:T(1,128)} %param.17) | copy-start | bytes 364
  11.9 37.3 %collective-permute-start.5 = (f32[3,1,1,64]{3,0,2,1:T(4,128)}, f32[3,1,1,64]{3,0,2,1:T(4,128)S(1)}, u32[]{:S(2)}, u32[]{:S(2)}) collective-permute-start(f32[3,1,1,64]{3,0,2,1:T(4,128)} %get-tuple-element.79), channel_id=1, source_target_pairs={{1,0},{3,2},{5,4},{7,6},{9,8},{11,10},{13,12},{15,14},{17,16},{19,... | collective-permute-start | bytes 2312 | tf_op jit(solution)/shard_map/ppermute | solution.py:22
  13.2 36.1 %collective-permute-start.4 = (f32[3,1,1,64]{3,0,2,1:T(4,128)}, f32[3,1,1,64]{3,0,2,1:T(4,128)}, u32[]{:S(2)}, u32[]{:S(2)}) collective-permute-start(f32[3,1,1,64]{3,0,2,1:T(4,128)} %get-tuple-element.78), channel_id=1, source_target_pairs={{0,1},{2,3},{4,5},{6,7},{8,9},{10,11},{12,13},{14,15},{16,17},{18,... | collective-permute-start | bytes 2312 | tf_op jit(solution)/shard_map/ppermute | solution.py:20
  50.0 6.3 %collective-permute-start.6 = (f32[3,1,26,64]{3,0,2,1:T(4,128)S(1)}, f32[3,1,26,64]{3,0,2,1:T(4,128)S(1)}, u32[]{:S(2)}, u32[]{:S(2)}) collective-permute-start(f32[3,1,26,64]{3,0,2,1:T(4,128)S(1)} %pad_maximum_fusion.8), channel_id=1, source_target_pairs={{0,2},{2,4},{4,6},{6,8},{8,10},{10,12},{12,14},{14,16},{16,18},{18... | collective-permute-start | bytes 59912 | tf_op jit(solution)/shard_map/ppermute | solution.py:31
  50.4 5.9 %collective-permute-start.8 = (f32[3,1,26,64]{3,0,2,1:T(4,128)S(1)}, f32[3,1,26,64]{3,0,2,1:T(4,128)S(1)}, u32[]{:S(2)}, u32[]{:S(2)}) collective-permute-start(f32[3,1,26,64]{3,0,2,1:T(4,128)S(1)} %pad_maximum_fusion.8), channel_id=1, source_target_pairs={{0,30},{2,0},{4,2},{6,4},{8,6},{10,8},{12,10},{14,12},{16,14},{18,... | collective-permute-start | bytes 59912 | tf_op jit(solution)/shard_map/ppermute | solution.py:31
  57.7 24.3 %collective-permute-start.7 = (f32[3,2,26,64]{3,0,2,1:T(4,128)}, f32[3,2,26,64]{3,0,2,1:T(4,128)S(1)}, u32[]{:S(2)}, u32[]{:S(2)}) collective-permute-start(f32[3,2,26,64]{3,0,2,1:T(4,128)} %get-tuple-element.76), channel_id=1, source_target_pairs={{0,4},{2,6},{4,8},{6,10},{8,12},{10,14},{12,16},{14,18},{16,20},{1... | collective-permute-start | bytes 119816 | tf_op jit(solution)/shard_map/ppermute | solution.py:31
  57.7 24.3 %collective-permute-start.9 = (f32[3,2,26,64]{3,0,2,1:T(4,128)S(1)}, f32[3,2,26,64]{3,0,2,1:T(4,128)S(1)}, u32[]{:S(2)}, u32[]{:S(2)}) collective-permute-start(f32[3,2,26,64]{3,0,2,1:T(4,128)S(1)} %get-tuple-element.77), channel_id=1, source_target_pairs={{0,28},{2,30},{4,0},{6,2},{8,4},{10,6},{12,8},{14,10},{16,12},{18,... | collective-permute-start | bytes 119816 | tf_op jit(solution)/shard_map/ppermute | solution.py:31
  63.1 22.8 %copy-start.2 = (f32[1,30,64,64]{3,2,1,0:T(8,128)S(1)}, f32[1,30,64,64]{3,2,1,0:T(8,128)}, u32[]{:S(2)}) copy-start(f32[1,30,64,64]{3,2,1,0:T(8,128)} %param.16) | copy-start | bytes 1474564
  82.8 11.7 %collective-permute-start.11 = (f32[3,4,26,64]{3,0,2,1:T(4,128)S(1)}, f32[3,4,26,64]{3,0,2,1:T(4,128)S(1)}, u32[]{:S(2)}, u32[]{:S(2)}) collective-permute-start(f32[3,4,26,64]{3,0,2,1:T(4,128)S(1)} %get-tuple-element.75), channel_id=1, source_target_pairs={{0,24},{2,26},{4,28},{6,30},{8,0},{10,2},{12,4},{14,6},{16,8},{18,... | collective-permute-start | bytes 239624 | tf_op jit(solution)/shard_map/ppermute | solution.py:31
  82.9 12.3 %collective-permute-start.10 = (f32[3,4,26,64]{3,0,2,1:T(4,128)S(1)}, f32[3,4,26,64]{3,0,2,1:T(4,128)S(1)}, u32[]{:S(2)}, u32[]{:S(2)}) collective-permute-start(f32[3,4,26,64]{3,0,2,1:T(4,128)S(1)} %get-tuple-element.74), channel_id=1, source_target_pairs={{0,8},{2,10},{4,12},{6,14},{8,16},{10,18},{12,20},{14,22},{16,24},... | collective-permute-start | bytes 239624 | tf_op jit(solution)/shard_map/ppermute | solution.py:31
  98.6 4.1 %collective-permute-start.3 = (f32[7,3,1,256]{3,0,2,1:T(8,128)S(1)}, f32[7,3,1,256]{3,0,2,1:T(8,128)S(1)}, u32[]{:S(2)}, u32[]{:S(2)}) collective-permute-start(f32[7,3,1,256]{3,0,2,1:T(8,128)S(1)} %get-tuple-element.32), channel_id=1, source_target_pairs={{1,0},{0,1},{3,2},{2,3},{5,4},{4,5},{7,6},{6,7},{9,8},{8,9},{11,10... | collective-permute-start | bytes 64520 | tf_op jit(solution)/shard_map/ppermute | solution.py:22
  100.6 3.9 %collective-permute-start.2 = (f32[7,3,1,256]{3,0,2,1:T(8,128)S(1)}, f32[7,3,1,256]{3,0,2,1:T(8,128)S(1)}, u32[]{:S(2)}, u32[]{:S(2)}) collective-permute-start(f32[7,3,1,256]{3,0,2,1:T(8,128)S(1)} %get-tuple-element.31), channel_id=1, source_target_pairs={{0,1},{1,0},{2,3},{3,2},{4,5},{5,4},{6,7},{7,6},{8,9},{9,8},{10,11... | collective-permute-start | bytes 64520 | tf_op jit(solution)/shard_map/ppermute | solution.py:20
  105.5 0.7 copy-start.10
  105.5 0.7 copy-start.11
  105.5 0.8 copy-start.12
  105.5 0.8 copy-start.13
  160.8 9.1 %copy-start.5 = (f32[3,1,24,256]{3,2,1,0:T(8,128)S(1)}, f32[3,1,24,256]{3,2,1,0:T(8,128)}, u32[]{:S(2)}) copy-start(f32[3,1,24,256]{3,2,1,0:T(8,128)} %param.10) | copy-start | bytes 221188
  160.8 9.1 %copy-start.9 = (f32[1,24,256]{2,1,0:T(8,128)S(1)}, f32[1,24,256]{2,1,0:T(8,128)}, u32[]{:S(2)}) copy-start(f32[1,24,256]{2,1,0:T(8,128)} %param.12) | copy-start | bytes 73732
where the time goes:
time: 191 us; the launch traced here: 190 us
  matrix products  97.9 us (51%)
  blocking collectives  25.5 us (13%)
  starting transfers between devices  25.3 us (13%)
  between operations  19.5 us (10%)
  waiting for transfers between devices  8.8 us (5%)
  local copies, waits for them, and re-layouts  6.93 us (4%)
  other arithmetic  6.05 us (3%)
    dot_general x9, matrix products, near_field(): jnp.einsum('alij,ralj->rali', kernel, source[4:], precision=HIGHEST_ACCUR...  82.1 us
    all_gather x1, blocking collectives, body(): every_sector = lax.all_gather(sector_coefs, 'blk', axis=1, tiled=True)  19.9 us
    ppermute x6, starting transfers between devices, passed_along(): return lax.ppermute(x, axis, [(i, (i + by) % count) for i in range(count)])  11.3 us
    ppermute x6, waiting for transfers between devices, passed_along(): return lax.ppermute(x, axis, [(i, (i + by) % count) for i in range(count)])  7.18 us
    dot_general x30, matrix products, add_sector(): jnp.einsum('skq,rslq->rslk', coupling, partner, precision=HIGHEST_ACCURACY)  7.17 us
    ppermute x3, starting transfers between devices, with_halo(): lax.ppermute(tail, axis, [(i, (i + 1) % count) for i in range(ends)])  7.16 us
    ppermute x3, starting transfers between devices, with_halo(): lax.ppermute(head, axis, [((i + 1) % count, i) for i in range(ends)])  6.83 us
    psum x1, blocking collectives, body(): sector_coefs = lax.psum(shared_portion, 'along')  5.63 us
  transfers between devices with their start and end apart: 12, of which 3 were waited for; matrix products, arithmetic and copies ran while one was open for 12% of the time, Pallas kernels for 0%

commit v1 on v0

--- a/solution.py
+++ b/solution.py
@@ -130,7 +130,15 @@
         precision=HIGHEST_ACCURACY,
     )
     sector_coefs = lax.psum(shared_portion, "along")
-    every_sector = lax.all_gather(sector_coefs, "blk", axis=1, tiled=True)
+    size = lax.axis_size("blk")
+    moving, blocks = (sector_coefs, [sector_coefs])
+    for _ in range(size - 1):
+        moving = lax.ppermute(moving, "blk", [(i_2, (i_2 + 1) % size) for i_2 in range(size)])
+        blocks.insert(0, moving)
+    row_of_blocks = jnp.concatenate(blocks, axis=1)
+    every_sector = jnp.roll(
+        row_of_blocks, (lax.axis_index("blk") + 1) * sector_coefs.shape[1], axis=1
+    )
     sector = lax.axis_index("blk")
     others = jnp.arange(sectors, dtype=jnp.int32)
     apart = (others - sector) % sectors

time: 191 us -> 240 us (1.26)
  waiting for transfers between devices: 8.8 us -> 58.5 us
  local copies, waits for them, and re-layouts: 6.93 us -> 27.4 us
  blocking collectives: 25.5 us -> 5.86 us
    ppermute x0 -> x15, waiting for transfers between devices: none -> 48.2 us  [body(): lax.ppermute(moving, 'blk', [(i_2, (i_2 + 1) % size) for i_2 in range(siz...]
    all_gather x1 -> x0, blocking collectives: 19.9 us -> none  [body(): every_sector = lax.all_gather(sector_coefs, 'blk', axis=1, tiled=True)]
    unnamed x46 -> x93, local copies, waits for them, and re-layouts: 2.66 us -> 22.4 us
  transfers between devices with their start and end apart: 12 -> 27, of which waited for: 3 -> 19; matrix products, arithmetic and copies ran while one was open for 12% -> 16% of each run, Pallas kernels for 0% -> 0%
where the time goes in v1:
time: 240 us; the launch traced here: 238 us
  matrix products  96.4 us (40%)
  waiting for transfers between devices  58.5 us (24%)
  local copies, waits for them, and re-layouts  27.4 us (11%)
  starting transfers between devices  24.5 us (10%)
  between operations  19.3 us (8%)
  other arithmetic  6.65 us (3%)
  blocking collectives  5.86 us (2%)
    dot_general x9, matrix products, near_field(): jnp.einsum('alij,ralj->rali', kernel, source[4:], precision=HIGHEST_ACCUR...  82.1 us
    ppermute x15, waiting for transfers between devices, body(): lax.ppermute(moving, 'blk', [(i_2, (i_2 + 1) % size) for i_2 in range(siz...  48.2 us
    unnamed x93, local copies, waits for them, and re-layouts  22.4 us
    ppermute x6, starting transfers between devices, passed_along(): return lax.ppermute(x, axis, [(i, (i + by) % count) for i in range(count)])  11.4 us
    ppermute x3, starting transfers between devices, with_halo(): lax.ppermute(head, axis, [((i + 1) % count, i) for i in range(ends)])  7.82 us
    ppermute x6, waiting for transfers between devices, passed_along(): return lax.ppermute(x, axis, [(i, (i + by) % count) for i in range(count)])  6.76 us
    dot_general x30, matrix products, add_sector(): jnp.einsum('skq,rslq->rslk', coupling, partner, precision=HIGHEST_ACCURACY)  6.41 us
    psum x1, blocking collectives, body(): sector_coefs = lax.psum(shared_portion, 'along')  5.86 us
  transfers between devices with their start and end apart: 27, of which 19 were waited for; matrix products, arithmetic and copies ran while one was open for 16% of the time, Pallas kernels for 0%

profile of v1, /device:TPU:0, one launch (start us, length us, event | category | flops | bytes accessed | tf_op | source)
XLA Modules:
  0.0 238.4 jit_solution(11362663102099953738)
XLA Ops:
  0.0 1.6 copy-done
  1.7 2.3 fusion.200
  4.6 5.9 %psum.7 = f32[3,1,64]{2,0,1:T(4,128)S(1)} all-reduce(f32[3,1,64]{2,0,1:T(4,128)S(1)} %convolution_bitcast_fusion.2), channel_id=1, replica_groups=mesh['blk'=16,'along'=2] {'along'}, use_global_device_ids=true, to_apply=%region_0.1 | all-reduce | flops 192 | bytes 1536 | tf_op jit(solution)/shard_map/psum | solution.py:132
  10.5 5.7 %collective-permute-done.12 = f32[3,1,64]{2,0,1:T(4,128)S(1)} collective-permute-done((f32[3,1,64]{2,0,1:T(4,128)S(1)}, f32[3,1,64]{2,0,1:T(4,128)S(1)}, u32[]{:S(2)}, u32[]{:S(2)}) %collective-permute-start.12) | collective-permute-done | bytes 800 | tf_op jit(solution)/shard_map/ppermute | solution.py:136
  16.3 5.5 %collective-permute-done.13 = f32[3,1,64]{2,0,1:T(4,128)S(1)} collective-permute-done((f32[3,1,64]{2,0,1:T(4,128)S(1)}, f32[3,1,64]{2,0,1:T(4,128)S(1)}, u32[]{:S(2)}, u32[]{:S(2)}) %collective-permute-start.13) | collective-permute-done | bytes 800 | tf_op jit(solution)/shard_map/ppermute | solution.py:136
  21.9 0.8 pad_maximum_fusion.4
  22.7 4.4 %collective-permute-start.1 = (f32[7,1,24,256]{3,0,2,1:T(8,128)}, f32[7,1,24,256]{3,0,2,1:T(8,128)S(1)}, u32[]{:S(2)}, u32[]{:S(2)}) collective-permute-start(f32[7,1,24,256]{3,0,2,1:T(8,128)} %pad_maximum_fusion.4), channel_id=1, source_target_pairs={{2,0},{4,2},{6,4},{8,6},{10,8},{12,10},{14,12},{16,14},{18,16},{20... | collective-permute-start | bytes 516104 | tf_op jit(solution)/shard_map/ppermute | solution.py:22
  28.2 1.3 collective-permute-start.5
  29.5 5.1 %collective-permute-start.4 = (f32[3,1,1,64]{3,0,2,1:T(4,128)}, f32[3,1,1,64]{3,0,2,1:T(4,128)}, u32[]{:S(2)}, u32[]{:S(2)}) collective-permute-start(f32[3,1,1,64]{3,0,2,1:T(4,128)} %get-tuple-element.78), channel_id=1, source_target_pairs={{0,1},{2,3},{4,5},{6,7},{8,9},{10,11},{12,13},{14,15},{16,17},{18,... | collective-permute-start | bytes 2312 | tf_op jit(solution)/shard_map/ppermute | solution.py:20
  35.7 1.4 slice_bitcast_fusion.48
  37.1 4.4 %collective-permute-done.16 = f32[3,1,64]{2,0,1:T(4,128)} collective-permute-done((f32[3,1,64]{2,0,1:T(4,128)S(1)}, f32[3,1,64]{2,0,1:T(4,128)}, u32[]{:S(2)}, u32[]{:S(2)}) %collective-permute-start.16) | collective-permute-done | bytes 800 | tf_op jit(solution)/shard_map/ppermute | solution.py:136
  41.5 1.3 broadcast_multiply_fusion
  42.9 4.7 %collective-permute-done.17 = f32[3,1,64]{2,0,1:T(4,128)} collective-permute-done((f32[3,1,64]{2,0,1:T(4,128)}, f32[3,1,64]{2,0,1:T(4,128)}, u32[]{:S(2)}, u32[]{:S(2)}) %collective-permute-start.17) | collective-permute-done | bytes 800 | tf_op jit(solution)/shard_map/ppermute | solution.py:136
  47.6 1.2 and_select_fusion
  48.7 4.7 %collective-permute-done.18 = f32[3,1,64]{2,0,1:T(4,128)S(1)} collective-permute-done((f32[3,1,64]{2,0,1:T(4,128)}, f32[3,1,64]{2,0,1:T(4,128)S(1)}, u32[]{:S(2)}, u32[]{:S(2)}) %collective-permute-start.18) | collective-permute-done | bytes 800 | tf_op jit(solution)/shard_map/ppermute | solution.py:136
  54.1 0.7 fusion.438
  54.8 5.1 %collective-permute-done.19 = f32[3,1,64]{2,0,1:T(4,128)} collective-permute-done((f32[3,1,64]{2,0,1:T(4,128)S(1)}, f32[3,1,64]{2,0,1:T(4,128)}, u32[]{:S(2)}, u32[]{:S(2)}) %collective-permute-start.19) | collective-permute-done | bytes 800 | tf_op jit(solution)/shard_map/ppermute | solution.py:136
  59.9 0.7 fusion.439
  60.6 5.3 %collective-permute-done.20 = f32[3,1,64]{2,0,1:T(4,128)} collective-permute-done((f32[3,1,64]{2,0,1:T(4,128)}, f32[3,1,64]{2,0,1:T(4,128)}, u32[]{:S(2)}, u32[]{:S(2)}) %collective-permute-start.20) | collective-permute-done | bytes 800 | tf_op jit(solution)/shard_map/ppermute | solution.py:136
  65.9 5.9 %collective-permute-done.21 = f32[3,1,64]{2,0,1:T(4,128)S(1)} collective-permute-done((f32[3,1,64]{2,0,1:T(4,128)}, f32[3,1,64]{2,0,1:T(4,128)S(1)}, u32[]{:S(2)}, u32[]{:S(2)}) %collective-permute-start.21) | collective-permute-done | bytes 800 | tf_op jit(solution)/shard_map/ppermute | solution.py:136
  76.2 1.4 collective-permute-done.22
  82.5 1.0 collective-permute-done.23
  89.1 0.8 collective-permute-done.24
  94.3 1.8 collective-permute-done.25
  96.1 0.7 pad_maximum_fusion.8
  96.8 4.5 %collective-permute-start.8 = (f32[3,1,26,64]{3,0,2,1:T(4,128)S(1)}, f32[3,1,26,64]{3,0,2,1:T(4,128)S(1)}, u32[]{:S(2)}, u32[]{:S(2)}) collective-permute-start(f32[3,1,26,64]{3,0,2,1:T(4,128)S(1)} %pad_maximum_fusion.8), channel_id=1, source_target_pairs={{0,30},{2,0},{4,2},{6,4},{8,6},{10,8},{12,10},{14,12},{16,14},{18,... | collective-permute-start | bytes 59912 | tf_op jit(solution)/shard_map/ppermute | solution.py:31
  102.0 0.7 constant_dynamic-update-slice_fusion.30
  102.7 0.7 constant_dynamic-update-slice_fusion.29
  104.0 0.7 constant_dynamic-update-slice_fusion.27
  105.4 0.7 constant_dynamic-update-slice_fusion.24
  106.1 0.7 constant_dynamic-update-slice_fusion.23
  108.1 0.7 constant_dynamic-update-slice_fusion.20
  109.5 0.7 constant_dynamic-update-slice_fusion.18
  110.2 0.7 constant_dynamic-update-slice_fusion.17
  110.8 0.7 constant_dynamic-update-slice_fusion.16
  111.5 0.7 constant_dynamic-update-slice_fusion.14
  112.2 0.7 constant_dynamic-update-slice_fusion.13
  113.6 0.7 constant_dynamic-update-slice_fusion.11
  114.9 0.7 constant_dynamic-update-slice_fusion.8
  115.6 0.7 constant_dynamic-update-slice_fusion.7
  117.7 0.7 constant_dynamic-update-slice_fusion.4
  119.7 0.7 constant_dynamic-update-slice_fusion.1
  120.4 0.7 constant_dynamic-update-slice_fusion
  121.1 1.2 convolution_bitcast_fusion
  122.3 0.7 pad_maximum_fusion.5
  123.1 4.7 %collective-permute-start.9 = (f32[3,2,26,64]{3,0,2,1:T(4,128)S(1)}, f32[3,2,26,64]{3,0,2,1:T(4,128)S(1)}, u32[]{:S(2)}, u32[]{:S(2)}) collective-permute-start(f32[3,2,26,64]{3,0,2,1:T(4,128)S(1)} %get-tuple-element.77), channel_id=1, source_target_pairs={{0,28},{2,30},{4,0},{6,2},{8,4},{10,6},{12,8},{14,10},{16,12},{18,... | collective-permute-start | bytes 119816 | tf_op jit(solution)/shard_map/ppermute | solution.py:31
  127.8 0.9 convolution_bitcast_fusion.1
  128.7 1.9 collective-permute-done.7
  130.7 0.8 pad_maximum_fusion.1
  131.9 1.6 collective-permute-start.10
  136.3 4.8 %collective-permute-done.11 = f32[3,4,26,64]{3,0,2,1:T(4,128)S(1)} collective-permute-done((f32[3,4,26,64]{3,0,2,1:T(4,128)S(1)}, f32[3,4,26,64]{3,0,2,1:T(4,128)S(1)}, u32[]{:S(2)}, u32[]{:S(2)}) %collective-permute-start.11) | collective-permute-done | bytes 79904 | tf_op jit(solution)/shard_map/ppermute | solution.py:31
  145.2 2.1 collective-permute-start.3
  147.3 1.9 convolution_add_fusion
  149.6 3.5 %collective-permute-done.2 = f32[7,3,1,256]{3,0,2,1:T(8,128)S(1)} collective-permute-done((f32[7,3,1,256]{3,0,2,1:T(8,128)S(1)}, f32[7,3,1,256]{3,0,2,1:T(8,128)S(1)}, u32[]{:S(2)}, u32[]{:S(2)}) %collective-permute-start.2) | collective-permute-done | bytes 21536 | tf_op jit(solution)/shard_map/ppermute | solution.py:20
  154.7 9.2 %fusion = f32[24,3,256]{2,1,0:T(4,128)S(1)} fusion(f32[24,256]{1,0:T(8,128)S(1)} %get-tuple-element.110, f32[24,256]{1,0:T(8,128)S(1)} %get-tuple-element.111, f32[24,256]{1,0:T(8,128)S(1)} %get-tuple-element.114, f32[24,256]{1,0:T(8,128)S(1)} %get-tuple-element.115, f32[24,256]{1,0:T(8,128)S(1)} %copy-done.12, f32[24,256]{1,0:T(8,128)S(1)} %copy-done.13, ...), kind=kOutput, calls=%fused_computation | convolution fusion | flops 73924608 | bytes 368640 | tf_op jit(solution)/shard_map/alij,ralj->rali/dot_general | solution.py:51
  164.0 9.1 %fusion.39 = f32[24,3,256]{2,1,0:T(4,128)S(1)} fusion(f32[24,256]{1,0:T(8,128)S(1)} %get-tuple-element.127, f32[24,256]{1,0:T(8,128)S(1)} %get-tuple-element.128, f32[24,256]{1,0:T(8,128)S(1)} %get-tuple-element.131, f32[24,256]{1,0:T(8,128)S(1)} %get-tuple-element.132, f32[24,256]{1,0:T(8,128)S(1)} %copy-done.12, f32[24,256]{1,0:T(8,128)S(1)} %copy-done.13, ...), kind=kOutput, calls=%fused_computation.39 | convolution fusion | flops 73924608 | bytes 368640 | tf_op jit(solution)/shard_map/alij,ralj->rali/dot_general | solution.py:51
  173.0 9.1 %fusion.26 = f32[24,3,256]{2,1,0:T(4,128)S(1)} fusion(f32[24,256]{1,0:T(8,128)S(1)} %get-tuple-element.118, f32[24,256]{1,0:T(8,128)S(1)} %get-tuple-element.119, f32[24,256]{1,0:T(8,128)S(1)} %get-tuple-element.122, f32[24,256]{1,0:T(8,128)S(1)} %get-tuple-element.123, f32[24,256]{1,0:T(8,128)S(1)} %copy-done.12, f32[24,256]{1,0:T(8,128)S(1)} %copy-done.13, ...), kind=kOutput, calls=%fused_computation.26 | convolution fusion | flops 73924608 | bytes 368640 | tf_op jit(solution)/shard_map/alij,ralj->rali/dot_general | solution.py:51
  182.1 9.1 %fusion.65 = f32[24,3,256]{2,1,0:T(4,128)S(1)} fusion(f32[24,256]{1,0:T(8,128)S(1)} %get-tuple-element.134, f32[24,256]{1,0:T(8,128)S(1)} %get-tuple-element.135, f32[24,256]{1,0:T(8,128)S(1)} %get-tuple-element.138, f32[24,256]{1,0:T(8,128)S(1)} %get-tuple-element.139, f32[24,256]{1,0:T(8,128)S(1)} %copy-done.12, f32[24,256]{1,0:T(8,128)S(1)} %copy-done.13, ...), kind=kOutput, calls=%fused_computation.65 | convolution fusion | flops 73924608 | bytes 368640 | tf_op jit(solution)/shard_map/alij,ralj->rali/dot_general | solution.py:51
  191.2 9.1 %fusion.78 = f32[24,3,256]{2,1,0:T(4,128)S(1)} fusion(f32[24,256]{1,0:T(8,128)S(1)} %get-tuple-element.133, f32[24,256]{1,0:T(8,128)S(1)} %get-tuple-element.129, f32[24,256]{1,0:T(8,128)S(1)} %get-tuple-element.117, f32[24,256]{1,0:T(8,128)S(1)} %get-tuple-element.113, f32[24,256]{1,0:T(8,128)S(1)} %copy-done.12, f32[24,256]{1,0:T(8,128)S(1)} %copy-done.13, ...), kind=kOutput, calls=%fused_computation.78 | convolution fusion | flops 73924608 | bytes 368640 | tf_op jit(solution)/shard_map/alij,ralj->rali/dot_general | solution.py:51
  200.2 9.1 %fusion.104 = f32[24,3,256]{2,1,0:T(4,128)S(1)} fusion(f32[24,256]{1,0:T(8,128)S(1)} %copy-done.12, f32[24,256]{1,0:T(8,128)S(1)} %get-tuple-element.141, f32[24,256]{1,0:T(8,128)S(1)} %copy-done.13, f32[24,256]{1,0:T(8,128)S(1)} %get-tuple-element.137, f32[24,256]{1,0:T(8,128)S(1)} %copy-done.11, f32[24,256]{1,0:T(8,128)S(1)} %get-tuple-element.125, ...), kind=kOutput, calls=%fused_computation.104 | convolution fusion | flops 73924608 | bytes 368640 | tf_op jit(solution)/shard_map/alij,ralj->rali/dot_general | solution.py:51
  209.3 9.1 %fusion.226 = f32[24,3,256]{2,1,0:T(4,128)S(1)} fusion(f32[24,3,256]{2,1,0:T(4,128)S(1)} %fusion.65, f32[24,3,256]{2,1,0:T(4,128)S(1)} %fusion.78, f32[24,3,256]{2,1,0:T(4,128)S(1)} %fusion.104, f32[24,256]{1,0:T(8,128)S(1)} %get-tuple-element.120, f32[24,256]{1,0:T(8,128)S(1)} %get-tuple-element.124, f32[24,256]{1,0:T(8,128)S(1)} %get-tuple-element.136, ...), kind=kOutput, calls=%fused_computation.210 | convolution fusion | flops 73979904 | bytes 663552 | tf_op jit(solution)/shard_map/alij,ralj->rali/dot_general | solution.py:51
  218.4 9.5 %fusion.217 = f32[24,3,256]{2,1,0:T(4,128)S(1)} fusion(f32[24,3,256]{2,1,0:T(4,128)S(1)} %fusion.26, f32[24,3,256]{2,1,0:T(4,128)S(1)} %fusion.39, f32[24,3,256]{2,1,0:T(4,128)S(1)} %fusion.226, f32[24,256]{1,0:T(8,128)S(1)} %copy-done.12, f32[24,256]{1,0:T(8,128)S(1)} %copy-done.13, f32[24,256]{1,0:T(8,128)S(1)} %copy-done.11, ...), kind=kOutput, calls=%fused_computation.207 | convolution fusion | flops 73979904 | bytes 491520 | tf_op jit(solution)/shard_map/alij,ralj->rali/dot_general | solution.py:51
  227.8 9.1 %fusion.232 = f32[24,3,256]{2,1,0:T(4,128)S(1)} fusion(f32[24,3,256]{2,1,0:T(4,128)S(1)} %fusion, f32[24,3,256]{2,1,0:T(4,128)S(1)} %fusion.217, f32[24,256]{1,0:T(8,128)S(1)} %get-tuple-element.112, f32[24,256]{1,0:T(8,128)S(1)} %get-tuple-element.116, f32[24,256]{1,0:T(8,128)S(1)} %get-tuple-element.126, f32[24,256]{1,0:T(8,128)S(1)} %get-tuple-element.130, ...), kind=kOutput, calls=%fused_computation.212 | convolution fusion | flops 73961472 | bytes 565248 | tf_op jit(solution)/shard_map/alij,ralj->rali/dot_general | solution.py:51
  236.9 0.9 fusion.205
  (159 shorter events, 22.0 us)
Async XLA Ops:
  0.0 1.7 copy-start
  0.0 16.2 %copy-start.5 = (f32[3,1,24,256]{3,2,1,0:T(8,128)S(1)}, f32[3,1,24,256]{3,2,1,0:T(8,128)}, u32[]{:S(2)}) copy-start(f32[3,1,24,256]{3,2,1,0:T(8,128)} %param.10) | copy-start | bytes 221188
  0.0 3.9 %copy-start.1 = (f32[1,24,64,64]{3,2,1,0:T(8,128)S(1)}, f32[1,24,64,64]{3,2,1,0:T(8,128)}, u32[]{:S(2)}) copy-start(f32[1,24,64,64]{3,2,1,0:T(8,128)} %param.14) | copy-start | bytes 1179652
  0.0 4.5 %copy-start.8 = (f32[1,1,64,64]{3,2,1,0:T(8,128)S(1)}, f32[1,1,64,64]{3,2,1,0:T(8,128)}, u32[]{:S(2)}) copy-start(f32[1,1,64,64]{3,2,1,0:T(8,128)} %param.15) | copy-start | bytes 49156
  0.0 16.2 %copy-start.9 = (f32[1,24,256]{2,1,0:T(8,128)S(1)}, f32[1,24,256]{2,1,0:T(8,128)}, u32[]{:S(2)}) copy-start(f32[1,24,256]{2,1,0:T(8,128)} %param.12) | copy-start | bytes 73732
  0.0 16.3 %copy-start.7 = (f32[3,1,24,256]{3,2,1,0:T(8,128)S(1)}, f32[3,1,24,256]{3,2,1,0:T(8,128)}, u32[]{:S(2)}) copy-start(f32[3,1,24,256]{3,2,1,0:T(8,128)} %param.11) | copy-start | bytes 221188
  1.7 52.4 %copy-start.4 = (s32[1,30]{1,0:T(1,128)S(1)}, s32[1,30]{1,0:T(1,128)}, u32[]{:S(2)}) copy-start(s32[1,30]{1,0:T(1,128)} %param.17) | copy-start | bytes 364
  3.9 117.2 %copy-start.3 = (f32[1,16,64,64]{3,2,1,0:T(8,128)S(1)}, f32[1,16,64,64]{3,2,1,0:T(8,128)}, u32[]{:S(2)}) copy-start(f32[1,16,64,64]{3,2,1,0:T(8,128)} %param.18) | copy-start | bytes 786436
  10.5 5.8 %copy-start.15 = (f32[3,1,64]{2,0,1:T(4,128)}, f32[3,1,64]{2,0,1:T(4,128)S(1)}, u32[]{:S(2)}) copy-start(f32[3,1,64]{2,0,1:T(4,128)S(1)} %psum.7) | copy-start | bytes 2308
  10.5 5.7 %collective-permute-start.12 = (f32[3,1,64]{2,0,1:T(4,128)S(1)}, f32[3,1,64]{2,0,1:T(4,128)S(1)}, u32[]{:S(2)}, u32[]{:S(2)}) collective-permute-start(f32[3,1,64]{2,0,1:T(4,128)S(1)} %psum.7), channel_id=1, source_target_pairs={{0,2},{2,4},{4,6},{6,8},{8,10},{10,12},{12,14},{14,16},{16,18},{18... | collective-permute-start | bytes 2312 | tf_op jit(solution)/shard_map/ppermute | solution.py:136
  16.2 5.7 %copy-start.16 = (f32[3,1,64]{2,0,1:T(4,128)}, f32[3,1,64]{2,0,1:T(4,128)S(1)}, u32[]{:S(2)}) copy-start(f32[3,1,64]{2,0,1:T(4,128)S(1)} %collective-permute-done.12) | copy-start | bytes 2308
  16.2 5.7 %collective-permute-start.13 = (f32[3,1,64]{2,0,1:T(4,128)S(1)}, f32[3,1,64]{2,0,1:T(4,128)S(1)}, u32[]{:S(2)}, u32[]{:S(2)}) collective-permute-start(f32[3,1,64]{2,0,1:T(4,128)S(1)} %collective-permute-done.12), channel_id=1, source_target_pairs={{0,2},{2,4},{4,6},{6,8},{8,10},{10,12},{12,14},{14,16},{16,18},{18... | collective-permute-start | bytes 2312 | tf_op jit(solution)/shard_map/ppermute | solution.py:136
  21.9 6.3 %copy-start.17 = (f32[3,1,64]{2,0,1:T(4,128)}, f32[3,1,64]{2,0,1:T(4,128)S(1)}, u32[]{:S(2)}) copy-start(f32[3,1,64]{2,0,1:T(4,128)S(1)} %collective-permute-done.13) | copy-start | bytes 2308
  21.9 5.7 %collective-permute-start.14 = (f32[3,1,64]{2,0,1:T(4,128)S(1)}, f32[3,1,64]{2,0,1:T(4,128)S(1)}, u32[]{:S(2)}, u32[]{:S(2)}) collective-permute-start(f32[3,1,64]{2,0,1:T(4,128)S(1)} %collective-permute-done.13), channel_id=1, source_target_pairs={{0,2},{2,4},{4,6},{6,8},{8,10},{10,12},{12,14},{14,16},{16,18},{18... | collective-permute-start | bytes 2312 | tf_op jit(solution)/shard_map/ppermute | solution.py:136
  22.7 122.5 %collective-permute-start.1 = (f32[7,1,24,256]{3,0,2,1:T(8,128)}, f32[7,1,24,256]{3,0,2,1:T(8,128)S(1)}, u32[]{:S(2)}, u32[]{:S(2)}) collective-permute-start(f32[7,1,24,256]{3,0,2,1:T(8,128)} %pad_maximum_fusion.4), channel_id=1, source_target_pairs={{2,0},{4,2},{6,4},{8,6},{10,8},{12,10},{14,12},{16,14},{18,16},{20... | collective-permute-start | bytes 516104 | tf_op jit(solution)/shard_map/ppermute | solution.py:22
  27.1 118.1 %collective-permute-start = (f32[7,1,24,256]{3,0,2,1:T(8,128)}, f32[7,1,24,256]{3,0,2,1:T(8,128)S(1)}, u32[]{:S(2)}, u32[]{:S(2)}) collective-permute-start(f32[7,1,24,256]{3,0,2,1:T(8,128)} %pad_maximum_fusion.4), channel_id=1, source_target_pairs={{0,2},{2,4},{4,6},{6,8},{8,10},{10,12},{12,14},{14,16},{16,18},{18... | collective-permute-start | bytes 516104 | tf_op jit(solution)/shard_map/ppermute | solution.py:20
  27.6 0.6 copy-start.18
  27.6 7.5 %collective-permute-start.15 = (f32[3,1,64]{2,0,1:T(4,128)S(1)}, f32[3,1,64]{2,0,1:T(4,128)S(1)}, u32[]{:S(2)}, u32[]{:S(2)}) collective-permute-start(f32[3,1,64]{2,0,1:T(4,128)S(1)} %collective-permute-done.14), channel_id=1, source_target_pairs={{0,2},{2,4},{4,6},{6,8},{8,10},{10,12},{12,14},{14,16},{16,18},{18... | collective-permute-start | bytes 2312 | tf_op jit(solution)/shard_map/ppermute | solution.py:136
  28.2 67.8 %collective-permute-start.5 = (f32[3,1,1,64]{3,0,2,1:T(4,128)}, f32[3,1,1,64]{3,0,2,1:T(4,128)S(1)}, u32[]{:S(2)}, u32[]{:S(2)}) collective-permute-start(f32[3,1,1,64]{3,0,2,1:T(4,128)} %get-tuple-element.79), channel_id=1, source_target_pairs={{1,0},{3,2},{5,4},{7,6},{9,8},{11,10},{13,12},{15,14},{17,16},{19,... | collective-permute-start | bytes 2312 | tf_op jit(solution)/shard_map/ppermute | solution.py:22
  29.5 66.6 %collective-permute-start.4 = (f32[3,1,1,64]{3,0,2,1:T(4,128)}, f32[3,1,1,64]{3,0,2,1:T(4,128)}, u32[]{:S(2)}, u32[]{:S(2)}) collective-permute-start(f32[3,1,1,64]{3,0,2,1:T(4,128)} %get-tuple-element.78), channel_id=1, source_target_pairs={{0,1},{2,3},{4,5},{6,7},{8,9},{10,11},{12,13},{14,15},{16,17},{18,... | collective-permute-start | bytes 2312 | tf_op jit(solution)/shard_map/ppermute | solution.py:20
  35.1 0.6 copy-start.19
  35.7 5.8 %collective-permute-start.16 = (f32[3,1,64]{2,0,1:T(4,128)S(1)}, f32[3,1,64]{2,0,1:T(4,128)}, u32[]{:S(2)}, u32[]{:S(2)}) collective-permute-start(f32[3,1,64]{2,0,1:T(4,128)S(1)} %collective-permute-done.15), channel_id=1, source_target_pairs={{0,2},{2,4},{4,6},{6,8},{8,10},{10,12},{12,14},{14,16},{16,18},{18... | collective-permute-start | bytes 2312 | tf_op jit(solution)/shard_map/ppermute | solution.py:136
  41.5 6.0 %collective-permute-start.17 = (f32[3,1,64]{2,0,1:T(4,128)}, f32[3,1,64]{2,0,1:T(4,128)}, u32[]{:S(2)}, u32[]{:S(2)}) collective-permute-start(f32[3,1,64]{2,0,1:T(4,128)} %collective-permute-done.16), channel_id=1, source_target_pairs={{0,2},{2,4},{4,6},{6,8},{8,10},{10,12},{12,14},{14,16},{16,18},{18... | collective-permute-start | bytes 2312 | tf_op jit(solution)/shard_map/ppermute | solution.py:136
  47.6 5.9 %collective-permute-start.18 = (f32[3,1,64]{2,0,1:T(4,128)}, f32[3,1,64]{2,0,1:T(4,128)S(1)}, u32[]{:S(2)}, u32[]{:S(2)}) collective-permute-start(f32[3,1,64]{2,0,1:T(4,128)} %collective-permute-done.17), channel_id=1, source_target_pairs={{0,2},{2,4},{4,6},{6,8},{8,10},{10,12},{12,14},{14,16},{16,18},{18... | collective-permute-start | bytes 2312 | tf_op jit(solution)/shard_map/ppermute | solution.py:136
  53.5 0.6 copy-start.20
  54.1 5.8 %collective-permute-start.19 = (f32[3,1,64]{2,0,1:T(4,128)S(1)}, f32[3,1,64]{2,0,1:T(4,128)}, u32[]{:S(2)}, u32[]{:S(2)}) collective-permute-start(f32[3,1,64]{2,0,1:T(4,128)S(1)} %collective-permute-done.18), channel_id=1, source_target_pairs={{0,2},{2,4},{4,6},{6,8},{8,10},{10,12},{12,14},{14,16},{16,18},{18... | collective-permute-start | bytes 2312 | tf_op jit(solution)/shard_map/ppermute | solution.py:136
  59.9 6.0 %collective-permute-start.20 = (f32[3,1,64]{2,0,1:T(4,128)}, f32[3,1,64]{2,0,1:T(4,128)}, u32[]{:S(2)}, u32[]{:S(2)}) collective-permute-start(f32[3,1,64]{2,0,1:T(4,128)} %collective-permute-done.19), channel_id=1, source_target_pairs={{0,2},{2,4},{4,6},{6,8},{8,10},{10,12},{12,14},{14,16},{16,18},{18... | collective-permute-start | bytes 2312 | tf_op jit(solution)/shard_map/ppermute | solution.py:136
  65.9 5.9 %collective-permute-start.21 = (f32[3,1,64]{2,0,1:T(4,128)}, f32[3,1,64]{2,0,1:T(4,128)S(1)}, u32[]{:S(2)}, u32[]{:S(2)}) collective-permute-start(f32[3,1,64]{2,0,1:T(4,128)} %collective-permute-done.20), channel_id=1, source_target_pairs={{0,2},{2,4},{4,6},{6,8},{8,10},{10,12},{12,14},{14,16},{16,18},{18... | collective-permute-start | bytes 2312 | tf_op jit(solution)/shard_map/ppermute | solution.py:136
  71.8 5.8 %collective-permute-start.22 = (f32[3,1,64]{2,0,1:T(4,128)S(1)}, f32[3,1,64]{2,0,1:T(4,128)}, u32[]{:S(2)}, u32[]{:S(2)}) collective-permute-start(f32[3,1,64]{2,0,1:T(4,128)S(1)} %collective-permute-done.21), channel_id=1, source_target_pairs={{0,2},{2,4},{4,6},{6,8},{8,10},{10,12},{12,14},{14,16},{16,18},{18... | collective-permute-start | bytes 2312 | tf_op jit(solution)/shard_map/ppermute | solution.py:136
  77.6 5.9 %collective-permute-start.23 = (f32[3,1,64]{2,0,1:T(4,128)}, f32[3,1,64]{2,0,1:T(4,128)S(1)}, u32[]{:S(2)}, u32[]{:S(2)}) collective-permute-start(f32[3,1,64]{2,0,1:T(4,128)} %collective-permute-done.22), channel_id=1, source_target_pairs={{0,2},{2,4},{4,6},{6,8},{8,10},{10,12},{12,14},{14,16},{16,18},{18... | collective-permute-start | bytes 2312 | tf_op jit(solution)/shard_map/ppermute | solution.py:136
  83.6 0.6 copy-start.21
  84.1 5.8 %collective-permute-start.24 = (f32[3,1,64]{2,0,1:T(4,128)S(1)}, f32[3,1,64]{2,0,1:T(4,128)}, u32[]{:S(2)}, u32[]{:S(2)}) collective-permute-start(f32[3,1,64]{2,0,1:T(4,128)S(1)} %collective-permute-done.23), channel_id=1, source_target_pairs={{0,2},{2,4},{4,6},{6,8},{8,10},{10,12},{12,14},{14,16},{16,18},{18... | collective-permute-start | bytes 2312 | tf_op jit(solution)/shard_map/ppermute | solution.py:136
  89.9 6.1 %collective-permute-start.25 = (f32[3,1,64]{2,0,1:T(4,128)}, f32[3,1,64]{2,0,1:T(4,128)}, u32[]{:S(2)}, u32[]{:S(2)}) collective-permute-start(f32[3,1,64]{2,0,1:T(4,128)} %collective-permute-done.24), channel_id=1, source_target_pairs={{0,2},{2,4},{4,6},{6,8},{8,10},{10,12},{12,14},{14,16},{16,18},{18... | collective-permute-start | bytes 2312 | tf_op jit(solution)/shard_map/ppermute | solution.py:136
  94.3 39.3 %copy-start.2 = (f32[1,30,64,64]{3,2,1,0:T(8,128)S(1)}, f32[1,30,64,64]{3,2,1,0:T(8,128)}, u32[]{:S(2)}) copy-start(f32[1,30,64,64]{3,2,1,0:T(8,128)} %param.16) | copy-start | bytes 1474564
  96.1 5.9 %collective-permute-start.26 = (f32[3,1,64]{2,0,1:T(4,128)}, f32[3,1,64]{2,0,1:T(4,128)S(1)}, u32[]{:S(2)}, u32[]{:S(2)}) collective-permute-start(f32[3,1,64]{2,0,1:T(4,128)} %collective-permute-done.25), channel_id=1, source_target_pairs={{0,2},{2,4},{4,6},{6,8},{8,10},{10,12},{12,14},{14,16},{16,18},{18... | collective-permute-start | bytes 2312 | tf_op jit(solution)/shard_map/ppermute | solution.py:136
  96.8 25.5 %collective-permute-start.6 = (f32[3,1,26,64]{3,0,2,1:T(4,128)S(1)}, f32[3,1,26,64]{3,0,2,1:T(4,128)S(1)}, u32[]{:S(2)}, u32[]{:S(2)}) collective-permute-start(f32[3,1,26,64]{3,0,2,1:T(4,128)S(1)} %pad_maximum_fusion.8), channel_id=1, source_target_pairs={{0,2},{2,4},{4,6},{6,8},{8,10},{10,12},{12,14},{14,16},{16,18},{18... | collective-permute-start | bytes 59912 | tf_op jit(solution)/shard_map/ppermute | solution.py:31
  96.8 25.5 %collective-permute-start.8 = (f32[3,1,26,64]{3,0,2,1:T(4,128)S(1)}, f32[3,1,26,64]{3,0,2,1:T(4,128)S(1)}, u32[]{:S(2)}, u32[]{:S(2)}) collective-permute-start(f32[3,1,26,64]{3,0,2,1:T(4,128)S(1)} %pad_maximum_fusion.8), channel_id=1, source_target_pairs={{0,30},{2,0},{4,2},{6,4},{8,6},{10,8},{12,10},{14,12},{16,14},{18,... | collective-permute-start | bytes 59912 | tf_op jit(solution)/shard_map/ppermute | solution.py:31
  123.0 7.6 %collective-permute-start.7 = (f32[3,2,26,64]{3,0,2,1:T(4,128)S(1)}, f32[3,2,26,64]{3,0,2,1:T(4,128)S(1)}, u32[]{:S(2)}, u32[]{:S(2)}) collective-permute-start(f32[3,2,26,64]{3,0,2,1:T(4,128)S(1)} %get-tuple-element.76), channel_id=1, source_target_pairs={{0,4},{2,6},{4,8},{6,10},{8,12},{10,14},{12,16},{14,18},{16,20},{1... | collective-permute-start | bytes 119816 | tf_op jit(solution)/shard_map/ppermute | solution.py:31
  123.1 7.6 %collective-permute-start.9 = (f32[3,2,26,64]{3,0,2,1:T(4,128)S(1)}, f32[3,2,26,64]{3,0,2,1:T(4,128)S(1)}, u32[]{:S(2)}, u32[]{:S(2)}) collective-permute-start(f32[3,2,26,64]{3,0,2,1:T(4,128)S(1)} %get-tuple-element.77), channel_id=1, source_target_pairs={{0,28},{2,30},{4,0},{6,2},{8,4},{10,6},{12,8},{14,10},{16,12},{18,... | collective-permute-start | bytes 119816 | tf_op jit(solution)/shard_map/ppermute | solution.py:31
  131.4 9.6 %collective-permute-start.11 = (f32[3,4,26,64]{3,0,2,1:T(4,128)S(1)}, f32[3,4,26,64]{3,0,2,1:T(4,128)S(1)}, u32[]{:S(2)}, u32[]{:S(2)}) collective-permute-start(f32[3,4,26,64]{3,0,2,1:T(4,128)S(1)} %get-tuple-element.75), channel_id=1, source_target_pairs={{0,24},{2,26},{4,28},{6,30},{8,0},{10,2},{12,4},{14,6},{16,8},{18,... | collective-permute-start | bytes 239624 | tf_op jit(solution)/shard_map/ppermute | solution.py:31
  131.9 9.9 %collective-permute-start.10 = (f32[3,4,26,64]{3,0,2,1:T(4,128)S(1)}, f32[3,4,26,64]{3,0,2,1:T(4,128)S(1)}, u32[]{:S(2)}, u32[]{:S(2)}) collective-permute-start(f32[3,4,26,64]{3,0,2,1:T(4,128)S(1)} %get-tuple-element.74), channel_id=1, source_target_pairs={{0,8},{2,10},{4,12},{6,14},{8,16},{10,18},{12,20},{14,22},{16,24},... | collective-permute-start | bytes 239624 | tf_op jit(solution)/shard_map/ppermute | solution.py:31
  145.2 4.1 %collective-permute-start.3 = (f32[7,3,1,256]{3,0,2,1:T(8,128)S(1)}, f32[7,3,1,256]{3,0,2,1:T(8,128)S(1)}, u32[]{:S(2)}, u32[]{:S(2)}) collective-permute-start(f32[7,3,1,256]{3,0,2,1:T(8,128)S(1)} %get-tuple-element.32), channel_id=1, source_target_pairs={{1,0},{0,1},{3,2},{2,3},{5,4},{4,5},{7,6},{6,7},{9,8},{8,9},{11,10... | collective-permute-start | bytes 64520 | tf_op jit(solution)/shard_map/ppermute | solution.py:22
  149.2 3.9 %collective-permute-start.2 = (f32[7,3,1,256]{3,0,2,1:T(8,128)S(1)}, f32[7,3,1,256]{3,0,2,1:T(8,128)S(1)}, u32[]{:S(2)}, u32[]{:S(2)}) collective-permute-start(f32[7,3,1,256]{3,0,2,1:T(8,128)S(1)} %get-tuple-element.31), channel_id=1, source_target_pairs={{0,1},{1,0},{2,3},{3,2},{4,5},{5,4},{6,7},{7,6},{8,9},{9,8},{10,11... | collective-permute-start | bytes 64520 | tf_op jit(solution)/shard_map/ppermute | solution.py:20
  154.0 0.7 copy-start.11
  154.0 0.7 copy-start.12
  154.0 0.8 copy-start.13
  154.0 0.8 copy-start.14
  209.3 9.1 %copy-start.6 = (f32[3,1,24,256]{3,2,1,0:T(8,128)S(1)}, f32[3,1,24,256]{3,2,1,0:T(8,128)}, u32[]{:S(2)}) copy-start(f32[3,1,24,256]{3,2,1,0:T(8,128)} %param.10) | copy-start | bytes 221188
  209.3 9.1 %copy-start.10 = (f32[1,24,256]{2,1,0:T(8,128)S(1)}, f32[1,24,256]{2,1,0:T(8,128)}, u32[]{:S(2)}) copy-start(f32[1,24,256]{2,1,0:T(8,128)} %param.12) | copy-start | bytes 73732
